TPU v7x, 32 devices: a whole 2x2x4 slice. The times are simulated.
32 devices in a mesh: mem: 8 (over y, x, core), col: 4 (over z).
Axes of the slice: x: 2, y: 2, z: 4, core: 2. Of those that a mesh axis runs over, the one named last changes fastest.
Arguments:
- background_trials: bfloat16 [256, 4, 32, 512], P('mem', None, None, 'col'), may hold values from -6 to 6
- region_active_tally: int32 [8, 16], P('mem', 'col'), may hold values from 256 to 2048, as said below
- sensed_component: int32 [8, 16, 2048], P('mem', 'col'), may hold values from 0 to 1919
- distance_bucket: int32 [8, 16, 2048], P('mem', 'col'), may hold values from 0 to 15
- sensor_readings: float32 [8, 16, 2048], P('mem', 'col'), may hold values from -6 to 6
- inverse_noise_variance: float32 [8, 16, 2048], P('mem', 'col'), may hold values from 0.25 to 4
- localization_factors: float32 [16], replicated, may hold values from 0.05 to 1
Outputs:
- analysis: bfloat16 [256, 4, 32, 512], P('mem', None, None, 'col')
Inputs may be any that keep to these rules, and one draw needn't show every extreme that they name: `region_active_tally`: observations of a patch fill its first slots; some patch has exactly 2048 live observations.
All inputs are finite; a program needn't handle non-finite values.
Results may differ from a plain program's by a relative error of at most 0.0063.
Values may be sent and summed in bfloat16 or wider, within the bound.
No kernel may reach another device: no remote copies, remote signals or barrier semaphores. Data moves between devices by JAX's collectives and lax.ppermute only.
A program may use at most 64 MiB of HBM per device.

v0:
```python
import jax
import jax.numpy as jnp
from jax import lax
from jax.sharding import PartitionSpec as P

SECTOR_SPAN = 32
REACH_MARGIN = 4
ITERS = 4
inflation = 1.1
obs_block = 128


def padded(block, sides, width):
    for axis, dim in sides:
        count = lax.axis_size(axis)
        forward = [(i, i + 1) for i in range(count - 1)]
        backward = [(target, source) for source, target in forward]
        low = lax.ppermute(
            lax.slice_in_dim(block, block.shape[dim] - width, None, axis=dim), axis, forward
        )
        high = lax.ppermute(lax.slice_in_dim(block, 0, width, axis=dim), axis, backward)
        block = jnp.concatenate([low, block, high], axis=dim)
    return block


def lookup(class_ids, weight_table):
    table_slots = jnp.arange(weight_table.shape[0], dtype=jnp.int32)
    return jnp.sum(jnp.where(class_ids[..., None] == table_slots, weight_table, 0.0), axis=-1)


def observe(
    anomaly_flat, average_flat, cell_ids, class_ids, values, inv_var, is_live, weight_table
):
    observed = jnp.take_along_axis(anomaly_flat, cell_ids[:, None, :], axis=2)
    innovation = values - jnp.take_along_axis(average_flat, cell_ids, axis=1)
    weight = jnp.where(is_live, inv_var * lookup(class_ids, weight_table), 0.0)
    scaled = (observed.astype(jnp.float32) * weight[:, None, :]).astype(jnp.bfloat16)
    gram_part = jnp.einsum("qkm,qjm->qkj", scaled, observed, preferred_element_type=jnp.float32)
    forcing_part = jnp.einsum(
        "qkm,qm->qk", scaled.astype(jnp.float32), innovation, precision=lax.Precision.HIGHEST
    )
    return (gram_part, forcing_part)


def local(
    background_trials,
    region_active_tally,
    sensed_component,
    distance_bucket,
    sensor_readings,
    inverse_noise_variance,
    localization_factors,
):
    local_region_tile = lax.all_to_all(
        background_trials, "mem", split_axis=2, concat_axis=0, tiled=True
    )
    enlarged_piece = padded(local_region_tile, (("mem", 2), ("col", 3)), REACH_MARGIN)
    trial_flattened = enlarged_piece.shape[0]
    physical_quantity_stack = enlarged_piece.shape[1]
    tile_height = enlarged_piece.shape[2] - 2 * REACH_MARGIN
    tile_width = enlarged_piece.shape[3] - 2 * REACH_MARGIN
    patches = tile_width // SECTOR_SPAN
    frame_breadth = SECTOR_SPAN + 2 * REACH_MARGIN
    unit_weights = jnp.ones((trial_flattened,), jnp.bfloat16)
    predicted_average = (
        lax.dot_general(
            unit_weights,
            enlarged_piece,
            (((0,), (0,)), ((), ())),
            preferred_element_type=jnp.float32,
        )
        / trial_flattened
    )
    deviation_matrix = (enlarged_piece.astype(jnp.float32) - predicted_average).astype(jnp.bfloat16)
    anomaly_flat = jnp.stack(
        [
            deviation_matrix[
                :, :, :, sector_index * SECTOR_SPAN : sector_index * SECTOR_SPAN + frame_breadth
            ]
            for sector_index in range(patches)
        ]
    ).reshape(patches, trial_flattened, -1)
    average_flat = jnp.stack(
        [
            predicted_average[
                :, :, sector_index * SECTOR_SPAN : sector_index * SECTOR_SPAN + frame_breadth
            ]
            for sector_index in range(patches)
        ]
    ).reshape(patches, -1)
    counts = region_active_tally.reshape(patches)
    cell_ids = sensed_component.reshape(patches, -1)
    class_ids = distance_bucket.reshape(patches, -1)
    values = sensor_readings.reshape(patches, -1)
    inv_vars = inverse_noise_variance.reshape(patches, -1)
    order_ids = jnp.broadcast_to(jnp.arange(cell_ids.shape[1], dtype=jnp.int32), cell_ids.shape)
    rounds = (jnp.max(counts) + obs_block - 1) // obs_block

    def one_round(round_id, partial_sums):
        block_start = round_id * obs_block

        def take_block(source):
            return lax.dynamic_slice_in_dim(source, block_start, obs_block, 1)

        gram_part, forcing_part = observe(
            anomaly_flat,
            average_flat,
            take_block(cell_ids),
            take_block(class_ids),
            take_block(values),
            take_block(inv_vars),
            take_block(order_ids) < counts[:, None],
            localization_factors,
        )
        return (partial_sums[0] + gram_part, partial_sums[1] + forcing_part)

    initial = (
        jnp.zeros((patches, trial_flattened, trial_flattened), jnp.float32),
        jnp.zeros((patches, trial_flattened), jnp.float32),
    )
    gram_sum, forcing = lax.fori_loop(0, rounds, one_round, initial)
    identity = jnp.eye(trial_flattened, dtype=jnp.float32)
    gram_sum = gram_sum + (trial_flattened - 1) / inflation * identity
    norm_scale = jnp.sqrt(jnp.sum(gram_sum * gram_sum, axis=(1, 2)))
    iterate = gram_sum / norm_scale[:, None, None]
    inverse_root = jnp.broadcast_to(identity, iterate.shape)
    for sweep_id in range(ITERS):
        factor = 1.5 * identity - 0.5 * jnp.einsum(
            "qij,qjk->qik", inverse_root, iterate, precision=lax.Precision.HIGHEST
        )
        if sweep_id + 1 < ITERS:
            iterate = jnp.einsum("qij,qjk->qik", iterate, factor, precision=lax.Precision.HIGHEST)
        inverse_root = jnp.einsum(
            "qij,qjk->qik", factor, inverse_root, precision=lax.Precision.HIGHEST
        )
    partial_shift = jnp.einsum("qij,qj->qi", inverse_root, forcing, precision=lax.Precision.HIGHEST)
    mean_shift = (
        jnp.einsum("qij,qj->qi", inverse_root, partial_shift, precision=lax.Precision.HIGHEST)
        / norm_scale[:, None]
    )
    spread_scale = jnp.sqrt((trial_flattened - 1.0) / norm_scale)
    transform = (spread_scale[:, None, None] * inverse_root + mean_shift[:, :, None]).astype(
        jnp.bfloat16
    )
    own_anomaly = deviation_matrix[
        :, :, REACH_MARGIN : REACH_MARGIN + tile_height, REACH_MARGIN : REACH_MARGIN + tile_width
    ].reshape(trial_flattened, physical_quantity_stack, tile_height, patches, SECTOR_SPAN)
    inner_midpoint = predicted_average[
        :, REACH_MARGIN : REACH_MARGIN + tile_height, REACH_MARGIN : REACH_MARGIN + tile_width
    ].reshape(physical_quantity_stack, tile_height, patches, SECTOR_SPAN)
    analysed = (
        jnp.einsum("kstqp,qkj->jstqp", own_anomaly, transform, preferred_element_type=jnp.float32)
        + inner_midpoint[None]
    )
    analysed = analysed.astype(jnp.bfloat16).reshape(
        trial_flattened, physical_quantity_stack, tile_height, tile_width
    )
    return lax.all_to_all(analysed, "mem", split_axis=0, concat_axis=2, tiled=True)


def solution(mesh):
    placed = (
        P("mem", None, None, "col"),
        P("mem", "col"),
        P("mem", "col", None),
        P("mem", "col", None),
        P("mem", "col", None),
        P("mem", "col", None),
        P(),
    )
    return jax.shard_map(
        local, mesh=mesh, in_specs=placed, out_specs=P("mem", None, None, "col"), check_vma=False
    )
```

profile of v0, /device:TPU:0, one launch (start us, length us, event | category | flops | bytes accessed | tf_op | source)
XLA Modules:
  0.0 388.7 jit_solution(7699056529408383022)
XLA Ops:
  0.0 1.9 copy.56
  1.9 20.3 %all_to_all.36 = bf16[32,4,32,128]{3,0,1,2:T(8,128)(2,1)S(1)} all-to-all(bf16[32,4,32,128]{3,0,1,2:T(8,128)(2,1)S(1)} %copy.56), channel_id=1, replica_groups=mesh['mem'=8,'col'=4] {'mem'}, dimensions={2} | all-to-all | bytes 2097152 | tf_op jit(solution)/shard_map/all_to_all | solution.py:54
  22.4 1.4 collective-permute-start
  23.7 1.3 collective-permute-start.1
  27.1 1.9 collective-permute-done.1
  30.4 3.0 fusion.34
  33.4 3.2 copy.59
  36.6 4.1 %collective-permute-start.2 = (bf16[256,4,12,4]{0,3,2,1:T(4,128)(2,1)S(1)}, bf16[256,4,12,4]{0,3,2,1:T(4,128)(2,1)}, u32[]{:S(2)}, u32[]{:S(2)}) collective-permute-start(bf16[256,4,12,4]{0,3,2,1:T(4,128)(2,1)S(1)} %copy.59), channel_id=1, source_target_pairs={{0,1},{1,2},{2,3},{4,5},{5,6},{6,7},{8,9},{9,10},{10,11},{12,13},{... | collective-permute-start | bytes 294920 | tf_op jit(solution)/shard_map/ppermute | solution.py:18
  40.8 2.1 copy.60
  42.9 1.5 collective-permute-start.3
  45.1 2.6 copy.61
  47.7 2.0 collective-permute-done.3
  49.7 3.6 copy.62
  53.3 7.1 %fusion.29 = f32[1,4,12,136]{3,0,2,1:T(1,128)S(1)} fusion(bf16[256,4,12,4]{3,0,2,1:T(8,128)(2,1)} %copy.62, bf16[256,4,4,128]{3,0,2,1:T(8,128)(2,1)} %copy-done.3, bf16[256,4,4,128]{3,0,2,1:T(8,128)(2,1)} %bitcast.95, bf16[256,4,4,128]{3,0,2,1:T(8,128)(2,1)} %copy-done.2, bf16[256,4,12,4]{3,0,2,1:T(8,128)(2,1)S(1)} %copy.61), kind=kOutput, calls=%fused_computation.60 | convolution fusion | flops 20054016 | bytes 3368448 | tf_op jit(solution)/shard_map/dot_general | solution.py:66
  63.6 8.0 %subtract_convert_fusion = bf16[256,4,12,136]{3,0,2,1:T(8,128)(2,1)S(1)} fusion(f32[4,12,136]{2,1,0:T(8,128)S(1)} %bitcast_multiply_fusion, bf16[256,4,12,4]{3,0,2,1:T(8,128)(2,1)} %copy.62, bf16[256,4,4,128]{3,0,2,1:T(8,128)(2,1)} %copy-done.3, bf16[256,4,4,128]{3,0,2,1:T(8,128)(2,1)} %bitcast.96, bf16[256,4,4,128]{3,0,2,1:T(8,128)(2,1)} %copy-done.2, ...), kind=kLoop, calls=%fused_computation.24 | loop fusion | flops 20054016 | bytes 6710784 | tf_op jit(solution)/shard_map/convert_element_type | solution.py:74
  71.6 5.4 %fusion.33 = (bf16[256,4,12,40]{3,0,2,1:T(8,128)(2,1)}, bf16[256,4,12,40]{3,0,2,1:T(8,128)(2,1)S(1)}, bf16[256,4,12,40]{3,0,2,1:T(8,128)(2,1)}, bf16[256,4,12,40]{3,0,2,1:T(8,128)(2,1)}) fusion(bf16[256,4,12,136]{3,0,2,1:T(8,128)(2,1)S(1)} %subtract_convert_fusion), kind=kLoop, calls=%fused_computation.65 | loop fusion | bytes 7864320 | tf_op jit(solution)/shard_map/slice | solution.py:77
  77.0 4.1 %copy.63 = bf16[256,4,12,40]{0,3,2,1:T(8,128)(2,1)} copy(bf16[256,4,12,40]{3,0,2,1:T(8,128)(2,1)} %get-tuple-element.105) | data formatting | bytes 1966080 | tf_op jit(solution)/shard_map/slice | solution.py:77
  81.1 4.1 %copy.64 = bf16[256,4,12,40]{0,3,2,1:T(8,128)(2,1)} copy(bf16[256,4,12,40]{3,0,2,1:T(8,128)(2,1)} %get-tuple-element.108) | data formatting | bytes 1966080 | tf_op jit(solution)/shard_map/slice | solution.py:77
  85.2 4.1 %copy.65 = bf16[256,4,12,40]{0,3,2,1:T(8,128)(2,1)} copy(bf16[256,4,12,40]{3,0,2,1:T(8,128)(2,1)} %get-tuple-element.107) | data formatting | bytes 1966080 | tf_op jit(solution)/shard_map/slice | solution.py:77
  89.2 2.2 copy.66
  91.5 3.7 pad_maximum_fusion.1
  95.3 234.1 %while.12 = (s32[]{:T(128)}, f32[4,256,256]{2,1,0:T(8,128)S(1)}, f32[4,256]{1,0:T(4,128)S(1)}, s32[]{:T(128)}, s32[4,2048]{1,0:T(4,128)}, /*index=5*/bf16[4,256,...) while((s32[]{:T(128)}, f32[4,256,256]{2,1,0:T(8,128)S(1)}, ...), condition=%wide.region_3.4_spmd, body=%wide.region_1.3_spmd.sunk | while | flops 70158344 | bytes 3735335 | solution.py:121
  96.1 4.8 %gather_fusion = f32[512]{0:T(512)S(1)} fusion(f32[4,1920]{1,0:T(4,128)S(1)} %get-tuple-element.251, s32[512]{0:T(512)S(1)} %fusion.67), kind=kCustom, calls=%fused_computation.1.clone.1 | custom fusion | bytes 8192 | tf_op jit(solution)/shard_map/while/body/jit(take_along_axis)/gather | solution.py:35
  102.5 6.6 %gather_fusion.1 = bf16[512,256]{1,0:T(8,128)(2,1)S(1)} fusion(bf16[4,256,1920]{1,2,0:T(8,128)(2,1)} %get-tuple-element.244, s32[512]{0:T(512)S(1)} %fusion.67), kind=kCustom, calls=%fused_computation.clone.1 | custom fusion | bytes 528384 | tf_op jit(solution)/shard_map/while/body/jit(take_along_axis)/gather | solution.py:34
  110.7 4.8 %gather_fusion = f32[512]{0:T(512)S(1)} fusion(f32[4,1920]{1,0:T(4,128)S(1)} %get-tuple-element.251, s32[512]{0:T(512)S(1)} %fusion.67), kind=kCustom, calls=%fused_computation.1.clone.1 | custom fusion | bytes 8192 | tf_op jit(solution)/shard_map/while/body/jit(take_along_axis)/gather | solution.py:35
  117.1 6.6 %gather_fusion.1 = bf16[512,256]{1,0:T(8,128)(2,1)S(1)} fusion(bf16[4,256,1920]{1,2,0:T(8,128)(2,1)} %get-tuple-element.244, s32[512]{0:T(512)S(1)} %fusion.67), kind=kCustom, calls=%fused_computation.clone.1 | custom fusion | bytes 528384 | tf_op jit(solution)/shard_map/while/body/jit(take_along_axis)/gather | solution.py:34
  125.4 4.8 %gather_fusion = f32[512]{0:T(512)S(1)} fusion(f32[4,1920]{1,0:T(4,128)S(1)} %get-tuple-element.251, s32[512]{0:T(512)S(1)} %fusion.67), kind=kCustom, calls=%fused_computation.1.clone.1 | custom fusion | bytes 8192 | tf_op jit(solution)/shard_map/while/body/jit(take_along_axis)/gather | solution.py:35
  131.8 6.6 %gather_fusion.1 = bf16[512,256]{1,0:T(8,128)(2,1)S(1)} fusion(bf16[4,256,1920]{1,2,0:T(8,128)(2,1)} %get-tuple-element.244, s32[512]{0:T(512)S(1)} %fusion.67), kind=kCustom, calls=%fused_computation.clone.1 | custom fusion | bytes 528384 | tf_op jit(solution)/shard_map/while/body/jit(take_along_axis)/gather | solution.py:34
  140.0 4.8 %gather_fusion = f32[512]{0:T(512)S(1)} fusion(f32[4,1920]{1,0:T(4,128)S(1)} %get-tuple-element.251, s32[512]{0:T(512)S(1)} %fusion.67), kind=kCustom, calls=%fused_computation.1.clone.1 | custom fusion | bytes 8192 | tf_op jit(solution)/shard_map/while/body/jit(take_along_axis)/gather | solution.py:35
  146.4 6.6 %gather_fusion.1 = bf16[512,256]{1,0:T(8,128)(2,1)S(1)} fusion(bf16[4,256,1920]{1,2,0:T(8,128)(2,1)} %get-tuple-element.244, s32[512]{0:T(512)S(1)} %fusion.67), kind=kCustom, calls=%fused_computation.clone.1 | custom fusion | bytes 528384 | tf_op jit(solution)/shard_map/while/body/jit(take_along_axis)/gather | solution.py:34
  154.6 4.8 %gather_fusion = f32[512]{0:T(512)S(1)} fusion(f32[4,1920]{1,0:T(4,128)S(1)} %get-tuple-element.251, s32[512]{0:T(512)S(1)} %fusion.67), kind=kCustom, calls=%fused_computation.1.clone.1 | custom fusion | bytes 8192 | tf_op jit(solution)/shard_map/while/body/jit(take_along_axis)/gather | solution.py:35
  161.0 6.6 %gather_fusion.1 = bf16[512,256]{1,0:T(8,128)(2,1)S(1)} fusion(bf16[4,256,1920]{1,2,0:T(8,128)(2,1)} %get-tuple-element.244, s32[512]{0:T(512)S(1)} %fusion.67), kind=kCustom, calls=%fused_computation.clone.1 | custom fusion | bytes 528384 | tf_op jit(solution)/shard_map/while/body/jit(take_along_axis)/gather | solution.py:34
  169.2 4.8 %gather_fusion = f32[512]{0:T(512)S(1)} fusion(f32[4,1920]{1,0:T(4,128)S(1)} %get-tuple-element.251, s32[512]{0:T(512)S(1)} %fusion.67), kind=kCustom, calls=%fused_computation.1.clone.1 | custom fusion | bytes 8192 | tf_op jit(solution)/shard_map/while/body/jit(take_along_axis)/gather | solution.py:35
  175.6 6.7 %gather_fusion.1 = bf16[512,256]{1,0:T(8,128)(2,1)S(1)} fusion(bf16[4,256,1920]{1,2,0:T(8,128)(2,1)} %get-tuple-element.244, s32[512]{0:T(512)S(1)} %fusion.67), kind=kCustom, calls=%fused_computation.clone.1 | custom fusion | bytes 528384 | tf_op jit(solution)/shard_map/while/body/jit(take_along_axis)/gather | solution.py:34
  183.9 4.8 %gather_fusion = f32[512]{0:T(512)S(1)} fusion(f32[4,1920]{1,0:T(4,128)S(1)} %get-tuple-element.251, s32[512]{0:T(512)S(1)} %fusion.67), kind=kCustom, calls=%fused_computation.1.clone.1 | custom fusion | bytes 8192 | tf_op jit(solution)/shard_map/while/body/jit(take_along_axis)/gather | solution.py:35
  190.3 6.6 %gather_fusion.1 = bf16[512,256]{1,0:T(8,128)(2,1)S(1)} fusion(bf16[4,256,1920]{1,2,0:T(8,128)(2,1)} %get-tuple-element.244, s32[512]{0:T(512)S(1)} %fusion.67), kind=kCustom, calls=%fused_computation.clone.1 | custom fusion | bytes 528384 | tf_op jit(solution)/shard_map/while/body/jit(take_along_axis)/gather | solution.py:34
  198.5 4.8 %gather_fusion = f32[512]{0:T(512)S(1)} fusion(f32[4,1920]{1,0:T(4,128)S(1)} %get-tuple-element.251, s32[512]{0:T(512)S(1)} %fusion.67), kind=kCustom, calls=%fused_computation.1.clone.1 | custom fusion | bytes 8192 | tf_op jit(solution)/shard_map/while/body/jit(take_along_axis)/gather | solution.py:35
  204.9 6.6 %gather_fusion.1 = bf16[512,256]{1,0:T(8,128)(2,1)S(1)} fusion(bf16[4,256,1920]{1,2,0:T(8,128)(2,1)} %get-tuple-element.244, s32[512]{0:T(512)S(1)} %fusion.67), kind=kCustom, calls=%fused_computation.clone.1 | custom fusion | bytes 528384 | tf_op jit(solution)/shard_map/while/body/jit(take_along_axis)/gather | solution.py:34
  213.1 4.8 %gather_fusion = f32[512]{0:T(512)S(1)} fusion(f32[4,1920]{1,0:T(4,128)S(1)} %get-tuple-element.251, s32[512]{0:T(512)S(1)} %fusion.67), kind=kCustom, calls=%fused_computation.1.clone.1 | custom fusion | bytes 8192 | tf_op jit(solution)/shard_map/while/body/jit(take_along_axis)/gather | solution.py:35
  219.5 6.6 %gather_fusion.1 = bf16[512,256]{1,0:T(8,128)(2,1)S(1)} fusion(bf16[4,256,1920]{1,2,0:T(8,128)(2,1)} %get-tuple-element.244, s32[512]{0:T(512)S(1)} %fusion.67), kind=kCustom, calls=%fused_computation.clone.1 | custom fusion | bytes 528384 | tf_op jit(solution)/shard_map/while/body/jit(take_along_axis)/gather | solution.py:34
  227.7 4.8 %gather_fusion = f32[512]{0:T(512)S(1)} fusion(f32[4,1920]{1,0:T(4,128)S(1)} %get-tuple-element.251, s32[512]{0:T(512)S(1)} %fusion.67), kind=kCustom, calls=%fused_computation.1.clone.1 | custom fusion | bytes 8192 | tf_op jit(solution)/shard_map/while/body/jit(take_along_axis)/gather | solution.py:35
  234.1 6.6 %gather_fusion.1 = bf16[512,256]{1,0:T(8,128)(2,1)S(1)} fusion(bf16[4,256,1920]{1,2,0:T(8,128)(2,1)} %get-tuple-element.244, s32[512]{0:T(512)S(1)} %fusion.67), kind=kCustom, calls=%fused_computation.clone.1 | custom fusion | bytes 528384 | tf_op jit(solution)/shard_map/while/body/jit(take_along_axis)/gather | solution.py:34
  242.3 4.8 %gather_fusion = f32[512]{0:T(512)S(1)} fusion(f32[4,1920]{1,0:T(4,128)S(1)} %get-tuple-element.251, s32[512]{0:T(512)S(1)} %fusion.67), kind=kCustom, calls=%fused_computation.1.clone.1 | custom fusion | bytes 8192 | tf_op jit(solution)/shard_map/while/body/jit(take_along_axis)/gather | solution.py:35
  248.7 6.6 %gather_fusion.1 = bf16[512,256]{1,0:T(8,128)(2,1)S(1)} fusion(bf16[4,256,1920]{1,2,0:T(8,128)(2,1)} %get-tuple-element.244, s32[512]{0:T(512)S(1)} %fusion.67), kind=kCustom, calls=%fused_computation.clone.1 | custom fusion | bytes 528384 | tf_op jit(solution)/shard_map/while/body/jit(take_along_axis)/gather | solution.py:34
  256.9 4.8 %gather_fusion = f32[512]{0:T(512)S(1)} fusion(f32[4,1920]{1,0:T(4,128)S(1)} %get-tuple-element.251, s32[512]{0:T(512)S(1)} %fusion.67), kind=kCustom, calls=%fused_computation.1.clone.1 | custom fusion | bytes 8192 | tf_op jit(solution)/shard_map/while/body/jit(take_along_axis)/gather | solution.py:35
  263.3 6.6 %gather_fusion.1 = bf16[512,256]{1,0:T(8,128)(2,1)S(1)} fusion(bf16[4,256,1920]{1,2,0:T(8,128)(2,1)} %get-tuple-element.244, s32[512]{0:T(512)S(1)} %fusion.67), kind=kCustom, calls=%fused_computation.clone.1 | custom fusion | bytes 528384 | tf_op jit(solution)/shard_map/while/body/jit(take_along_axis)/gather | solution.py:34
  271.5 4.8 %gather_fusion = f32[512]{0:T(512)S(1)} fusion(f32[4,1920]{1,0:T(4,128)S(1)} %get-tuple-element.251, s32[512]{0:T(512)S(1)} %fusion.67), kind=kCustom, calls=%fused_computation.1.clone.1 | custom fusion | bytes 8192 | tf_op jit(solution)/shard_map/while/body/jit(take_along_axis)/gather | solution.py:35
  277.9 6.6 %gather_fusion.1 = bf16[512,256]{1,0:T(8,128)(2,1)S(1)} fusion(bf16[4,256,1920]{1,2,0:T(8,128)(2,1)} %get-tuple-element.244, s32[512]{0:T(512)S(1)} %fusion.67), kind=kCustom, calls=%fused_computation.clone.1 | custom fusion | bytes 528384 | tf_op jit(solution)/shard_map/while/body/jit(take_along_axis)/gather | solution.py:34
  286.1 4.8 %gather_fusion = f32[512]{0:T(512)S(1)} fusion(f32[4,1920]{1,0:T(4,128)S(1)} %get-tuple-element.251, s32[512]{0:T(512)S(1)} %fusion.67), kind=kCustom, calls=%fused_computation.1.clone.1 | custom fusion | bytes 8192 | tf_op jit(solution)/shard_map/while/body/jit(take_along_axis)/gather | solution.py:35
  292.5 6.6 %gather_fusion.1 = bf16[512,256]{1,0:T(8,128)(2,1)S(1)} fusion(bf16[4,256,1920]{1,2,0:T(8,128)(2,1)} %get-tuple-element.244, s32[512]{0:T(512)S(1)} %fusion.67), kind=kCustom, calls=%fused_computation.clone.1 | custom fusion | bytes 528384 | tf_op jit(solution)/shard_map/while/body/jit(take_along_axis)/gather | solution.py:34
  300.8 4.8 %gather_fusion = f32[512]{0:T(512)S(1)} fusion(f32[4,1920]{1,0:T(4,128)S(1)} %get-tuple-element.251, s32[512]{0:T(512)S(1)} %fusion.67), kind=kCustom, calls=%fused_computation.1.clone.1 | custom fusion | bytes 8192 | tf_op jit(solution)/shard_map/while/body/jit(take_along_axis)/gather | solution.py:35
  307.2 6.6 %gather_fusion.1 = bf16[512,256]{1,0:T(8,128)(2,1)S(1)} fusion(bf16[4,256,1920]{1,2,0:T(8,128)(2,1)} %get-tuple-element.244, s32[512]{0:T(512)S(1)} %fusion.67), kind=kCustom, calls=%fused_computation.clone.1 | custom fusion | bytes 528384 | tf_op jit(solution)/shard_map/while/body/jit(take_along_axis)/gather | solution.py:34
  315.4 4.8 %gather_fusion = f32[512]{0:T(512)S(1)} fusion(f32[4,1920]{1,0:T(4,128)S(1)} %get-tuple-element.251, s32[512]{0:T(512)S(1)} %fusion.67), kind=kCustom, calls=%fused_computation.1.clone.1 | custom fusion | bytes 8192 | tf_op jit(solution)/shard_map/while/body/jit(take_along_axis)/gather | solution.py:35
  321.8 6.6 %gather_fusion.1 = bf16[512,256]{1,0:T(8,128)(2,1)S(1)} fusion(bf16[4,256,1920]{1,2,0:T(8,128)(2,1)} %get-tuple-element.244, s32[512]{0:T(512)S(1)} %fusion.67), kind=kCustom, calls=%fused_computation.clone.1 | custom fusion | bytes 528384 | tf_op jit(solution)/shard_map/while/body/jit(take_along_axis)/gather | solution.py:34
  329.7 1.2 fusion.13
  331.0 1.2 fusion.32
  333.3 1.2 fusion.12
  334.5 1.1 fusion.37
  336.8 1.2 fusion.11
  338.0 1.1 fusion.39
  340.3 2.0 slice.62
  342.4 1.5 fusion.10
  349.5 37.4 %all_to_all.37 = bf16[256,4,4,128]{3,2,1,0:T(4,128)(2,1)S(1)} all-to-all(bf16[256,4,4,128]{3,2,1,0:T(4,128)(2,1)S(1)} %copy.71), channel_id=1, replica_groups=mesh['mem'=8,'col'=4] {'mem'}, dimensions={0} | all-to-all | bytes 2097152 | tf_op jit(solution)/shard_map/all_to_all | solution.py:158
  387.3 1.4 copy.74
  (184 shorter events, 66.7 us)
Async XLA Ops:
  0.0 25.0 %copy-start.7 = (s32[1,4]{1,0:T(1,128)S(1)}, s32[1,4]{1,0:T(1,128)}, u32[]{:S(2)}) copy-start(s32[1,4]{1,0:T(1,128)} %param.10) | copy-start | bytes 52
  22.4 6.7 %copy-start.1 = (bf16[8,32,4,4,128]{4,1,0,3,2:T(8,128)(2,1)}, bf16[8,32,4,4,128]{4,1,0,3,2:T(8,128)(2,1)S(1)}, u32[]{:S(2)}) copy-start(bf16[8,32,4,4,128]{4,1,0,3,2:T(8,128)(2,1)S(1)} %copy.58) | copy-start | bytes 3145732
  22.4 4.7 %collective-permute-start = (bf16[256,4,4,128]{3,0,2,1:T(8,128)(2,1)S(1)}, bf16[256,4,4,128]{3,0,2,1:T(8,128)(2,1)S(1)}, u32[]{:S(2)}, u32[]{:S(2)}) collective-permute-start(bf16[256,4,4,128]{3,0,2,1:T(8,128)(2,1)S(1)} %bitcast.92), channel_id=1, source_target_pairs={{0,4},{4,8},{8,12},{12,16},{16,20},{20,24},{24,28},{1,5},{5,9},{9,... | collective-permute-start | bytes 3145736 | tf_op jit(solution)/shard_map/ppermute | solution.py:18
  23.7 5.3 %collective-permute-start.1 = (bf16[256,4,4,128]{3,0,2,1:T(8,128)(2,1)S(1)}, bf16[256,4,4,128]{3,0,2,1:T(8,128)(2,1)S(1)}, u32[]{:S(2)}, u32[]{:S(2)}) collective-permute-start(bf16[256,4,4,128]{3,0,2,1:T(8,128)(2,1)S(1)} %bitcast.93), channel_id=1, source_target_pairs={{4,0},{8,4},{12,8},{16,12},{20,16},{24,20},{28,24},{5,1},{9,5},{13... | collective-permute-start | bytes 3145736 | tf_op jit(solution)/shard_map/ppermute | solution.py:21
  27.1 1.9 copy-start.2
  29.0 1.0 copy-start.3
  36.6 8.5 %collective-permute-start.2 = (bf16[256,4,12,4]{0,3,2,1:T(4,128)(2,1)S(1)}, bf16[256,4,12,4]{0,3,2,1:T(4,128)(2,1)}, u32[]{:S(2)}, u32[]{:S(2)}) collective-permute-start(bf16[256,4,12,4]{0,3,2,1:T(4,128)(2,1)S(1)} %copy.59), channel_id=1, source_target_pairs={{0,1},{1,2},{2,3},{4,5},{5,6},{6,7},{8,9},{9,10},{10,11},{12,13},{... | collective-permute-start | bytes 294920 | tf_op jit(solution)/shard_map/ppermute | solution.py:18
  42.9 6.8 %collective-permute-start.3 = (bf16[256,4,12,4]{0,3,2,1:T(4,128)(2,1)}, bf16[256,4,12,4]{0,3,2,1:T(4,128)(2,1)}, u32[]{:S(2)}, u32[]{:S(2)}) collective-permute-start(bf16[256,4,12,4]{0,3,2,1:T(4,128)(2,1)} %copy.60), channel_id=1, source_target_pairs={{1,0},{2,1},{3,2},{5,4},{6,5},{7,6},{9,8},{10,9},{11,10},{13,12},{... | collective-permute-start | bytes 294920 | tf_op jit(solution)/shard_map/ppermute | solution.py:21
  71.6 5.4 %copy-start = (bf16[256,4,12,136]{3,0,2,1:T(8,128)(2,1)}, bf16[256,4,12,136]{3,0,2,1:T(8,128)(2,1)S(1)}, u32[]{:S(2)}) copy-start(bf16[256,4,12,136]{3,0,2,1:T(8,128)(2,1)S(1)} %subtract_convert_fusion) | copy-start | bytes 10027012
  85.2 6.3 %copy-start.6 = (f32[1,1920]{1,0:T(1,128)S(1)}, f32[1,1920]{1,0:T(1,128)}, u32[]{:S(2)}) copy-start(f32[1,1920]{1,0:T(1,128)} %stack.37) | copy-start | bytes 23044
  91.5 3.8 copy-start.8
  91.5 3.8 copy-start.9
  95.3 234.2 %copy-start.4 = (f32[256,256]{1,0:T(8,128)S(1)}, f32[256,256]{1,0:T(8,128)}, u32[]{:S(2)}) copy-start(f32[256,256]{1,0:T(8,128)} %get-tuple-element.118) | copy-start | bytes 786436
  95.3 234.4 %copy-start.5 = (f32[256,256]{1,0:T(8,128)S(1)}, f32[256,256]{1,0:T(8,128)}, u32[]{:S(2)}) copy-start(f32[256,256]{1,0:T(8,128)} %fusion.22) | copy-start | bytes 786436
where the time goes:
time: 392 us; the launch traced here: 389 us
  local copies, waits for them, and re-layouts  243 us (62%)
  blocking collectives  57.8 us (15%)
  other arithmetic  39.9 us (10%)
  matrix products  33.8 us (9%)
  starting transfers between devices  8.24 us (2%)
  waiting for transfers between devices  3.97 us (1%)
    gather x32, local copies, waits for them, and re-layouts, observe(): observed = jnp.take_along_axis(anomaly_flat, cell_ids[:, None, :], axis=2)  108 us
    gather x16, local copies, waits for them, and re-layouts, observe(): innovation = values - jnp.take_along_axis(average_flat, cell_ids, axis=1)  77.3 us
    all_to_all x1, blocking collectives, local(): lax.all_to_all(analysed, 'mem', split_axis=0, concat_axis=2, tiled=True)  37.4 us
    all_to_all x1, blocking collectives, local(): lax.all_to_all(background_trials, 'mem', split_axis=2, concat_axis=0, til...  20.3 us
    slice x5, local copies, waits for them, and re-layouts, local(): deviation_matrix[:, :, :, sector_index * SECTOR_SPAN:sector_index * SECTO...  19.8 us
    sub x16, other arithmetic, observe(): innovation = values - jnp.take_along_axis(average_flat, cell_ids, axis=1)  12.5 us
    gather x16, other arithmetic, observe(): observed = jnp.take_along_axis(anomaly_flat, cell_ids[:, None, :], axis=2)  11.2 us
    dynamic_slice x16, local copies, waits for them, and re-layouts, take_block(): return lax.dynamic_slice_in_dim(source, block_start, obs_block, 1)  11 us
  transfers between devices with their start and end apart: 4, of which 2 were waited for; matrix products, arithmetic and copies ran while one was open for 2% of the time, Pallas kernels for 0%

commit v1 on v0

--- a/solution.py
+++ b/solution.py
@@ -155,7 +155,10 @@
     analysed = analysed.astype(jnp.bfloat16).reshape(
         trial_flattened, physical_quantity_stack, tile_height, tile_width
     )
-    return lax.all_to_all(analysed, "mem", split_axis=0, concat_axis=2, tiled=True)
+    return jnp.concatenate(
+        lax.all_to_all(jnp.stack(jnp.split(analysed, lax.axis_size("mem"), axis=0)), "mem", 0, 0),
+        axis=2,
+    )
 
 
 def solution(mesh):

time: 392 us -> 411 us (1.048)
  local copies, waits for them, and re-layouts: 243 us -> 258 us
    split x0 -> x9, local copies, waits for them, and re-layouts: none -> 8.96 us  [local(): jnp.split(analysed, lax.axis_size('mem'), axis=0)]
    another operation x0 -> x9, local copies, waits for them, and re-layouts: none -> 6.89 us  [local(): jnp.stack(jnp.split(analysed, lax.axis_size('mem'), axis=0))]
where the time goes in v1:
time: 411 us; the launch traced here: 404 us
  local copies, waits for them, and re-layouts  258 us (63%)
  blocking collectives  57.6 us (14%)
  other arithmetic  39.9 us (10%)
  matrix products  33.7 us (8%)
  starting transfers between devices  8.52 us (2%)
    gather x32, local copies, waits for them, and re-layouts, observe(): observed = jnp.take_along_axis(anomaly_flat, cell_ids[:, None, :], axis=2)  109 us
    gather x16, local copies, waits for them, and re-layouts, observe(): innovation = values - jnp.take_along_axis(average_flat, cell_ids, axis=1)  77.3 us
    all_to_all x1, blocking collectives, local(): lax.all_to_all(jnp.stack(jnp.split(analysed, lax.axis_size('mem'), axis=0...  37.3 us
    all_to_all x1, blocking collectives, local(): lax.all_to_all(background_trials, 'mem', split_axis=2, concat_axis=0, til...  20.3 us
    slice x5, local copies, waits for them, and re-layouts, local(): deviation_matrix[:, :, :, sector_index * SECTOR_SPAN:sector_index * SECTO...  19.9 us
    sub x16, other arithmetic, observe(): innovation = values - jnp.take_along_axis(average_flat, cell_ids, axis=1)  12.5 us
    gather x16, other arithmetic, observe(): observed = jnp.take_along_axis(anomaly_flat, cell_ids[:, None, :], axis=2)  11.2 us
    dynamic_slice x16, local copies, waits for them, and re-layouts, take_block(): return lax.dynamic_slice_in_dim(source, block_start, obs_block, 1)  11 us
  transfers between devices with their start and end apart: 4, of which 2 were waited for; matrix products, arithmetic and copies ran while one was open for 2% of the time, Pallas kernels for 0%

profile of v1, /device:TPU:0, one launch (start us, length us, event | category | flops | bytes accessed | tf_op | source)
XLA Modules:
  0.0 404.2 jit_solution(6175401384580795290)
XLA Ops:
  0.0 1.9 copy.73
  1.9 20.3 %all_to_all.23 = bf16[32,4,32,128]{3,0,1,2:T(8,128)(2,1)S(1)} all-to-all(bf16[32,4,32,128]{3,0,1,2:T(8,128)(2,1)S(1)} %copy.73), channel_id=1, replica_groups=mesh['mem'=8,'col'=4] {'mem'}, dimensions={2} | all-to-all | bytes 2097152 | tf_op jit(solution)/shard_map/all_to_all | solution.py:54
  22.4 1.4 collective-permute-start
  23.7 1.3 collective-permute-start.1
  27.1 1.9 collective-permute-done.1
  30.4 3.0 fusion.34
  33.4 3.2 copy.76
  36.7 4.1 %collective-permute-start.2 = (bf16[256,4,12,4]{0,3,2,1:T(4,128)(2,1)S(1)}, bf16[256,4,12,4]{0,3,2,1:T(4,128)(2,1)}, u32[]{:S(2)}, u32[]{:S(2)}) collective-permute-start(bf16[256,4,12,4]{0,3,2,1:T(4,128)(2,1)S(1)} %copy.76), channel_id=1, source_target_pairs={{0,1},{1,2},{2,3},{4,5},{5,6},{6,7},{8,9},{9,10},{10,11},{12,13},{... | collective-permute-start | bytes 294920 | tf_op jit(solution)/shard_map/ppermute | solution.py:18
  40.8 2.1 copy.77
  42.9 1.7 collective-permute-start.3
  45.4 2.6 copy.78
  48.0 1.8 collective-permute-done.3
  49.7 3.6 copy.79
  53.3 7.1 %fusion.29 = f32[1,4,12,136]{3,0,2,1:T(1,128)S(1)} fusion(bf16[256,4,12,4]{3,0,2,1:T(8,128)(2,1)} %copy.79, bf16[256,4,4,128]{3,0,2,1:T(8,128)(2,1)} %copy-done.3, bf16[256,4,4,128]{3,0,2,1:T(8,128)(2,1)} %bitcast.108, bf16[256,4,4,128]{3,0,2,1:T(8,128)(2,1)} %copy-done.2, bf16[256,4,12,4]{3,0,2,1:T(8,128)(2,1)S(1)} %copy.78), kind=kOutput, calls=%fused_computation.68 | convolution fusion | flops 20054016 | bytes 3368448 | tf_op jit(solution)/shard_map/dot_general | solution.py:66
  63.6 8.0 %subtract_convert_fusion = bf16[256,4,12,136]{3,0,2,1:T(8,128)(2,1)S(1)} fusion(f32[4,12,136]{2,1,0:T(8,128)S(1)} %bitcast_multiply_fusion, bf16[256,4,12,4]{3,0,2,1:T(8,128)(2,1)} %copy.79, bf16[256,4,4,128]{3,0,2,1:T(8,128)(2,1)} %copy-done.3, bf16[256,4,4,128]{3,0,2,1:T(8,128)(2,1)} %bitcast.109, bf16[256,4,4,128]{3,0,2,1:T(8,128)(2,1)} %copy-done.2, ...), kind=kLoop, calls=%fused_computation.24 | loop fusion | flops 20054016 | bytes 6710784 | tf_op jit(solution)/shard_map/convert_element_type | solution.py:74
  71.6 5.4 %fusion.33 = (bf16[256,4,12,40]{3,0,2,1:T(8,128)(2,1)}, bf16[256,4,12,40]{3,0,2,1:T(8,128)(2,1)S(1)}, bf16[256,4,12,40]{3,0,2,1:T(8,128)(2,1)}, bf16[256,4,12,40]{3,0,2,1:T(8,128)(2,1)}) fusion(bf16[256,4,12,136]{3,0,2,1:T(8,128)(2,1)S(1)} %subtract_convert_fusion), kind=kLoop, calls=%fused_computation.73 | loop fusion | bytes 7864320 | tf_op jit(solution)/shard_map/slice | solution.py:77
  77.1 4.1 %copy.80 = bf16[256,4,12,40]{0,3,2,1:T(8,128)(2,1)} copy(bf16[256,4,12,40]{3,0,2,1:T(8,128)(2,1)} %get-tuple-element.105) | data formatting | bytes 1966080 | tf_op jit(solution)/shard_map/slice | solution.py:77
  81.1 4.1 %copy.81 = bf16[256,4,12,40]{0,3,2,1:T(8,128)(2,1)} copy(bf16[256,4,12,40]{3,0,2,1:T(8,128)(2,1)} %get-tuple-element.108) | data formatting | bytes 1966080 | tf_op jit(solution)/shard_map/slice | solution.py:77
  85.2 4.1 %copy.82 = bf16[256,4,12,40]{0,3,2,1:T(8,128)(2,1)} copy(bf16[256,4,12,40]{3,0,2,1:T(8,128)(2,1)} %get-tuple-element.107) | data formatting | bytes 1966080 | tf_op jit(solution)/shard_map/slice | solution.py:77
  89.3 2.2 copy.83
  91.6 3.7 pad_maximum_fusion.1
  95.4 234.3 %while.12 = (s32[]{:T(128)}, f32[4,256,256]{2,1,0:T(8,128)S(1)}, f32[4,256]{1,0:T(4,128)S(1)}, s32[]{:T(128)}, s32[4,2048]{1,0:T(4,128)}, /*index=5*/bf16[4,256,...) while((s32[]{:T(128)}, f32[4,256,256]{2,1,0:T(8,128)S(1)}, ...), condition=%wide.region_3.4_spmd, body=%wide.region_1.3_spmd.sunk | while | flops 70158344 | bytes 3735335 | solution.py:121
  96.2 4.8 %gather_fusion = f32[512]{0:T(512)S(1)} fusion(f32[4,1920]{1,0:T(4,128)S(1)} %get-tuple-element.259, s32[512]{0:T(512)S(1)} %fusion.68), kind=kCustom, calls=%fused_computation.1.clone.1 | custom fusion | bytes 8192 | tf_op jit(solution)/shard_map/while/body/jit(take_along_axis)/gather | solution.py:35
  102.6 6.6 %gather_fusion.1 = bf16[512,256]{1,0:T(8,128)(2,1)S(1)} fusion(bf16[4,256,1920]{1,2,0:T(8,128)(2,1)} %get-tuple-element.252, s32[512]{0:T(512)S(1)} %fusion.68), kind=kCustom, calls=%fused_computation.clone.1 | custom fusion | bytes 528384 | tf_op jit(solution)/shard_map/while/body/jit(take_along_axis)/gather | solution.py:34
  110.8 4.8 %gather_fusion = f32[512]{0:T(512)S(1)} fusion(f32[4,1920]{1,0:T(4,128)S(1)} %get-tuple-element.259, s32[512]{0:T(512)S(1)} %fusion.68), kind=kCustom, calls=%fused_computation.1.clone.1 | custom fusion | bytes 8192 | tf_op jit(solution)/shard_map/while/body/jit(take_along_axis)/gather | solution.py:35
  117.2 6.6 %gather_fusion.1 = bf16[512,256]{1,0:T(8,128)(2,1)S(1)} fusion(bf16[4,256,1920]{1,2,0:T(8,128)(2,1)} %get-tuple-element.252, s32[512]{0:T(512)S(1)} %fusion.68), kind=kCustom, calls=%fused_computation.clone.1 | custom fusion | bytes 528384 | tf_op jit(solution)/shard_map/while/body/jit(take_along_axis)/gather | solution.py:34
  125.4 4.8 %gather_fusion = f32[512]{0:T(512)S(1)} fusion(f32[4,1920]{1,0:T(4,128)S(1)} %get-tuple-element.259, s32[512]{0:T(512)S(1)} %fusion.68), kind=kCustom, calls=%fused_computation.1.clone.1 | custom fusion | bytes 8192 | tf_op jit(solution)/shard_map/while/body/jit(take_along_axis)/gather | solution.py:35
  131.8 6.7 %gather_fusion.1 = bf16[512,256]{1,0:T(8,128)(2,1)S(1)} fusion(bf16[4,256,1920]{1,2,0:T(8,128)(2,1)} %get-tuple-element.252, s32[512]{0:T(512)S(1)} %fusion.68), kind=kCustom, calls=%fused_computation.clone.1 | custom fusion | bytes 528384 | tf_op jit(solution)/shard_map/while/body/jit(take_along_axis)/gather | solution.py:34
  140.1 4.8 %gather_fusion = f32[512]{0:T(512)S(1)} fusion(f32[4,1920]{1,0:T(4,128)S(1)} %get-tuple-element.259, s32[512]{0:T(512)S(1)} %fusion.68), kind=kCustom, calls=%fused_computation.1.clone.1 | custom fusion | bytes 8192 | tf_op jit(solution)/shard_map/while/body/jit(take_along_axis)/gather | solution.py:35
  146.5 6.6 %gather_fusion.1 = bf16[512,256]{1,0:T(8,128)(2,1)S(1)} fusion(bf16[4,256,1920]{1,2,0:T(8,128)(2,1)} %get-tuple-element.252, s32[512]{0:T(512)S(1)} %fusion.68), kind=kCustom, calls=%fused_computation.clone.1 | custom fusion | bytes 528384 | tf_op jit(solution)/shard_map/while/body/jit(take_along_axis)/gather | solution.py:34
  154.7 4.8 %gather_fusion = f32[512]{0:T(512)S(1)} fusion(f32[4,1920]{1,0:T(4,128)S(1)} %get-tuple-element.259, s32[512]{0:T(512)S(1)} %fusion.68), kind=kCustom, calls=%fused_computation.1.clone.1 | custom fusion | bytes 8192 | tf_op jit(solution)/shard_map/while/body/jit(take_along_axis)/gather | solution.py:35
  161.1 6.6 %gather_fusion.1 = bf16[512,256]{1,0:T(8,128)(2,1)S(1)} fusion(bf16[4,256,1920]{1,2,0:T(8,128)(2,1)} %get-tuple-element.252, s32[512]{0:T(512)S(1)} %fusion.68), kind=kCustom, calls=%fused_computation.clone.1 | custom fusion | bytes 528384 | tf_op jit(solution)/shard_map/while/body/jit(take_along_axis)/gather | solution.py:34
  169.3 4.8 %gather_fusion = f32[512]{0:T(512)S(1)} fusion(f32[4,1920]{1,0:T(4,128)S(1)} %get-tuple-element.259, s32[512]{0:T(512)S(1)} %fusion.68), kind=kCustom, calls=%fused_computation.1.clone.1 | custom fusion | bytes 8192 | tf_op jit(solution)/shard_map/while/body/jit(take_along_axis)/gather | solution.py:35
  175.7 6.6 %gather_fusion.1 = bf16[512,256]{1,0:T(8,128)(2,1)S(1)} fusion(bf16[4,256,1920]{1,2,0:T(8,128)(2,1)} %get-tuple-element.252, s32[512]{0:T(512)S(1)} %fusion.68), kind=kCustom, calls=%fused_computation.clone.1 | custom fusion | bytes 528384 | tf_op jit(solution)/shard_map/while/body/jit(take_along_axis)/gather | solution.py:34
  184.0 4.8 %gather_fusion = f32[512]{0:T(512)S(1)} fusion(f32[4,1920]{1,0:T(4,128)S(1)} %get-tuple-element.259, s32[512]{0:T(512)S(1)} %fusion.68), kind=kCustom, calls=%fused_computation.1.clone.1 | custom fusion | bytes 8192 | tf_op jit(solution)/shard_map/while/body/jit(take_along_axis)/gather | solution.py:35
  190.4 6.6 %gather_fusion.1 = bf16[512,256]{1,0:T(8,128)(2,1)S(1)} fusion(bf16[4,256,1920]{1,2,0:T(8,128)(2,1)} %get-tuple-element.252, s32[512]{0:T(512)S(1)} %fusion.68), kind=kCustom, calls=%fused_computation.clone.1 | custom fusion | bytes 528384 | tf_op jit(solution)/shard_map/while/body/jit(take_along_axis)/gather | solution.py:34
  198.6 4.8 %gather_fusion = f32[512]{0:T(512)S(1)} fusion(f32[4,1920]{1,0:T(4,128)S(1)} %get-tuple-element.259, s32[512]{0:T(512)S(1)} %fusion.68), kind=kCustom, calls=%fused_computation.1.clone.1 | custom fusion | bytes 8192 | tf_op jit(solution)/shard_map/while/body/jit(take_along_axis)/gather | solution.py:35
  205.0 6.6 %gather_fusion.1 = bf16[512,256]{1,0:T(8,128)(2,1)S(1)} fusion(bf16[4,256,1920]{1,2,0:T(8,128)(2,1)} %get-tuple-element.252, s32[512]{0:T(512)S(1)} %fusion.68), kind=kCustom, calls=%fused_computation.clone.1 | custom fusion | bytes 528384 | tf_op jit(solution)/shard_map/while/body/jit(take_along_axis)/gather | solution.py:34
  213.2 4.8 %gather_fusion = f32[512]{0:T(512)S(1)} fusion(f32[4,1920]{1,0:T(4,128)S(1)} %get-tuple-element.259, s32[512]{0:T(512)S(1)} %fusion.68), kind=kCustom, calls=%fused_computation.1.clone.1 | custom fusion | bytes 8192 | tf_op jit(solution)/shard_map/while/body/jit(take_along_axis)/gather | solution.py:35
  219.6 6.6 %gather_fusion.1 = bf16[512,256]{1,0:T(8,128)(2,1)S(1)} fusion(bf16[4,256,1920]{1,2,0:T(8,128)(2,1)} %get-tuple-element.252, s32[512]{0:T(512)S(1)} %fusion.68), kind=kCustom, calls=%fused_computation.clone.1 | custom fusion | bytes 528384 | tf_op jit(solution)/shard_map/while/body/jit(take_along_axis)/gather | solution.py:34
  227.8 4.8 %gather_fusion = f32[512]{0:T(512)S(1)} fusion(f32[4,1920]{1,0:T(4,128)S(1)} %get-tuple-element.259, s32[512]{0:T(512)S(1)} %fusion.68), kind=kCustom, calls=%fused_computation.1.clone.1 | custom fusion | bytes 8192 | tf_op jit(solution)/shard_map/while/body/jit(take_along_axis)/gather | solution.py:35
  234.2 6.6 %gather_fusion.1 = bf16[512,256]{1,0:T(8,128)(2,1)S(1)} fusion(bf16[4,256,1920]{1,2,0:T(8,128)(2,1)} %get-tuple-element.252, s32[512]{0:T(512)S(1)} %fusion.68), kind=kCustom, calls=%fused_computation.clone.1 | custom fusion | bytes 528384 | tf_op jit(solution)/shard_map/while/body/jit(take_along_axis)/gather | solution.py:34
  242.5 4.8 %gather_fusion = f32[512]{0:T(512)S(1)} fusion(f32[4,1920]{1,0:T(4,128)S(1)} %get-tuple-element.259, s32[512]{0:T(512)S(1)} %fusion.68), kind=kCustom, calls=%fused_computation.1.clone.1 | custom fusion | bytes 8192 | tf_op jit(solution)/shard_map/while/body/jit(take_along_axis)/gather | solution.py:35
  248.9 6.6 %gather_fusion.1 = bf16[512,256]{1,0:T(8,128)(2,1)S(1)} fusion(bf16[4,256,1920]{1,2,0:T(8,128)(2,1)} %get-tuple-element.252, s32[512]{0:T(512)S(1)} %fusion.68), kind=kCustom, calls=%fused_computation.clone.1 | custom fusion | bytes 528384 | tf_op jit(solution)/shard_map/while/body/jit(take_along_axis)/gather | solution.py:34
  257.1 4.8 %gather_fusion = f32[512]{0:T(512)S(1)} fusion(f32[4,1920]{1,0:T(4,128)S(1)} %get-tuple-element.259, s32[512]{0:T(512)S(1)} %fusion.68), kind=kCustom, calls=%fused_computation.1.clone.1 | custom fusion | bytes 8192 | tf_op jit(solution)/shard_map/while/body/jit(take_along_axis)/gather | solution.py:35
  263.5 6.6 %gather_fusion.1 = bf16[512,256]{1,0:T(8,128)(2,1)S(1)} fusion(bf16[4,256,1920]{1,2,0:T(8,128)(2,1)} %get-tuple-element.252, s32[512]{0:T(512)S(1)} %fusion.68), kind=kCustom, calls=%fused_computation.clone.1 | custom fusion | bytes 528384 | tf_op jit(solution)/shard_map/while/body/jit(take_along_axis)/gather | solution.py:34
  271.7 4.8 %gather_fusion = f32[512]{0:T(512)S(1)} fusion(f32[4,1920]{1,0:T(4,128)S(1)} %get-tuple-element.259, s32[512]{0:T(512)S(1)} %fusion.68), kind=kCustom, calls=%fused_computation.1.clone.1 | custom fusion | bytes 8192 | tf_op jit(solution)/shard_map/while/body/jit(take_along_axis)/gather | solution.py:35
  278.1 6.6 %gather_fusion.1 = bf16[512,256]{1,0:T(8,128)(2,1)S(1)} fusion(bf16[4,256,1920]{1,2,0:T(8,128)(2,1)} %get-tuple-element.252, s32[512]{0:T(512)S(1)} %fusion.68), kind=kCustom, calls=%fused_computation.clone.1 | custom fusion | bytes 528384 | tf_op jit(solution)/shard_map/while/body/jit(take_along_axis)/gather | solution.py:34
  286.3 4.8 %gather_fusion = f32[512]{0:T(512)S(1)} fusion(f32[4,1920]{1,0:T(4,128)S(1)} %get-tuple-element.259, s32[512]{0:T(512)S(1)} %fusion.68), kind=kCustom, calls=%fused_computation.1.clone.1 | custom fusion | bytes 8192 | tf_op jit(solution)/shard_map/while/body/jit(take_along_axis)/gather | solution.py:35
  292.7 6.6 %gather_fusion.1 = bf16[512,256]{1,0:T(8,128)(2,1)S(1)} fusion(bf16[4,256,1920]{1,2,0:T(8,128)(2,1)} %get-tuple-element.252, s32[512]{0:T(512)S(1)} %fusion.68), kind=kCustom, calls=%fused_computation.clone.1 | custom fusion | bytes 528384 | tf_op jit(solution)/shard_map/while/body/jit(take_along_axis)/gather | solution.py:34
  301.0 4.8 %gather_fusion = f32[512]{0:T(512)S(1)} fusion(f32[4,1920]{1,0:T(4,128)S(1)} %get-tuple-element.259, s32[512]{0:T(512)S(1)} %fusion.68), kind=kCustom, calls=%fused_computation.1.clone.1 | custom fusion | bytes 8192 | tf_op jit(solution)/shard_map/while/body/jit(take_along_axis)/gather | solution.py:35
  307.4 6.6 %gather_fusion.1 = bf16[512,256]{1,0:T(8,128)(2,1)S(1)} fusion(bf16[4,256,1920]{1,2,0:T(8,128)(2,1)} %get-tuple-element.252, s32[512]{0:T(512)S(1)} %fusion.68), kind=kCustom, calls=%fused_computation.clone.1 | custom fusion | bytes 528384 | tf_op jit(solution)/shard_map/while/body/jit(take_along_axis)/gather | solution.py:34
  315.6 4.8 %gather_fusion = f32[512]{0:T(512)S(1)} fusion(f32[4,1920]{1,0:T(4,128)S(1)} %get-tuple-element.259, s32[512]{0:T(512)S(1)} %fusion.68), kind=kCustom, calls=%fused_computation.1.clone.1 | custom fusion | bytes 8192 | tf_op jit(solution)/shard_map/while/body/jit(take_along_axis)/gather | solution.py:35
  322.0 6.6 %gather_fusion.1 = bf16[512,256]{1,0:T(8,128)(2,1)S(1)} fusion(bf16[4,256,1920]{1,2,0:T(8,128)(2,1)} %get-tuple-element.252, s32[512]{0:T(512)S(1)} %fusion.68), kind=kCustom, calls=%fused_computation.clone.1 | custom fusion | bytes 528384 | tf_op jit(solution)/shard_map/while/body/jit(take_along_axis)/gather | solution.py:34
  340.5 2.0 slice.70
  342.6 1.4 fusion.10
  348.4 2.2 fusion.35
  350.6 2.1 copy.87
  352.7 1.4 stack.67
  354.7 2.1 copy.88
  356.8 1.4 stack.68
  359.3 1.4 stack.69
  365.2 37.3 %all_to_all.24 = bf16[8,32,4,4,128]{4,1,3,2,0:T(8,128)(2,1)S(1)} all-to-all(bf16[8,32,4,4,128]{4,1,3,2,0:T(8,128)(2,1)S(1)} %constant_dynamic-update-slice_fusion), channel_id=1, replica_groups=mesh['mem'=8,'col'=4] {'mem'}, dimensions={0} | all-to-all | bytes 2097152 | tf_op jit(solution)/shard_map/all_to_all | solution.py:159
  402.6 1.4 copy.96
  (212 shorter events, 78.4 us)
Async XLA Ops:
  0.0 25.0 %copy-start.10 = (s32[1,4]{1,0:T(1,128)S(1)}, s32[1,4]{1,0:T(1,128)}, u32[]{:S(2)}) copy-start(s32[1,4]{1,0:T(1,128)} %param.10) | copy-start | bytes 52
  22.4 6.7 %copy-start.1 = (bf16[8,32,4,4,128]{4,1,0,3,2:T(8,128)(2,1)}, bf16[8,32,4,4,128]{4,1,0,3,2:T(8,128)(2,1)S(1)}, u32[]{:S(2)}) copy-start(bf16[8,32,4,4,128]{4,1,0,3,2:T(8,128)(2,1)S(1)} %copy.75) | copy-start | bytes 3145732
  22.4 4.7 %collective-permute-start = (bf16[256,4,4,128]{3,0,2,1:T(8,128)(2,1)S(1)}, bf16[256,4,4,128]{3,0,2,1:T(8,128)(2,1)S(1)}, u32[]{:S(2)}, u32[]{:S(2)}) collective-permute-start(bf16[256,4,4,128]{3,0,2,1:T(8,128)(2,1)S(1)} %bitcast.105), channel_id=1, source_target_pairs={{0,4},{4,8},{8,12},{12,16},{16,20},{20,24},{24,28},{1,5},{5,9},{9,... | collective-permute-start | bytes 3145736 | tf_op jit(solution)/shard_map/ppermute | solution.py:18
  23.7 5.3 %collective-permute-start.1 = (bf16[256,4,4,128]{3,0,2,1:T(8,128)(2,1)S(1)}, bf16[256,4,4,128]{3,0,2,1:T(8,128)(2,1)S(1)}, u32[]{:S(2)}, u32[]{:S(2)}) collective-permute-start(bf16[256,4,4,128]{3,0,2,1:T(8,128)(2,1)S(1)} %bitcast.106), channel_id=1, source_target_pairs={{4,0},{8,4},{12,8},{16,12},{20,16},{24,20},{28,24},{5,1},{9,5},{13... | collective-permute-start | bytes 3145736 | tf_op jit(solution)/shard_map/ppermute | solution.py:21
  27.1 1.9 copy-start.2
  29.0 1.0 copy-start.3
  36.7 8.7 %collective-permute-start.2 = (bf16[256,4,12,4]{0,3,2,1:T(4,128)(2,1)S(1)}, bf16[256,4,12,4]{0,3,2,1:T(4,128)(2,1)}, u32[]{:S(2)}, u32[]{:S(2)}) collective-permute-start(bf16[256,4,12,4]{0,3,2,1:T(4,128)(2,1)S(1)} %copy.76), channel_id=1, source_target_pairs={{0,1},{1,2},{2,3},{4,5},{5,6},{6,7},{8,9},{9,10},{10,11},{12,13},{... | collective-permute-start | bytes 294920 | tf_op jit(solution)/shard_map/ppermute | solution.py:18
  42.9 6.8 %collective-permute-start.3 = (bf16[256,4,12,4]{0,3,2,1:T(4,128)(2,1)}, bf16[256,4,12,4]{0,3,2,1:T(4,128)(2,1)}, u32[]{:S(2)}, u32[]{:S(2)}) collective-permute-start(bf16[256,4,12,4]{0,3,2,1:T(4,128)(2,1)} %copy.77), channel_id=1, source_target_pairs={{1,0},{2,1},{3,2},{5,4},{6,5},{7,6},{9,8},{10,9},{11,10},{13,12},{... | collective-permute-start | bytes 294920 | tf_op jit(solution)/shard_map/ppermute | solution.py:21
  71.6 5.4 %copy-start = (bf16[256,4,12,136]{3,0,2,1:T(8,128)(2,1)}, bf16[256,4,12,136]{3,0,2,1:T(8,128)(2,1)S(1)}, u32[]{:S(2)}) copy-start(bf16[256,4,12,136]{3,0,2,1:T(8,128)(2,1)S(1)} %subtract_convert_fusion) | copy-start | bytes 10027012
  85.2 6.3 %copy-start.9 = (f32[1,1920]{1,0:T(1,128)S(1)}, f32[1,1920]{1,0:T(1,128)}, u32[]{:S(2)}) copy-start(f32[1,1920]{1,0:T(1,128)} %stack.64) | copy-start | bytes 23044
  91.6 3.8 copy-start.11
  91.6 3.8 copy-start.12
  95.4 234.3 %copy-start.5 = (f32[256,256]{1,0:T(8,128)S(1)}, f32[256,256]{1,0:T(8,128)}, u32[]{:S(2)}) copy-start(f32[256,256]{1,0:T(8,128)} %get-tuple-element.126) | copy-start | bytes 786436
  95.4 234.5 %copy-start.6 = (f32[256,256]{1,0:T(8,128)S(1)}, f32[256,256]{1,0:T(8,128)}, u32[]{:S(2)}) copy-start(f32[256,256]{1,0:T(8,128)} %fusion.22) | copy-start | bytes 786436
  362.6 2.5 copy-start.4
  363.8 1.3 copy-start.7
  363.8 1.3 copy-start.8
